TPU v7x, 32 devices: a whole 2x2x4 slice. The times are simulated.
32 devices in a mesh: dp: 4 (over y, core), mp: 8 (over z, x).
Axes of the slice: x: 2, y: 2, z: 4, core: 2. Of those that a mesh axis runs over, the one named last changes fastest.
Arguments:
- layer_input: bfloat16 [128, 256, 768], P(('dp', 'mp')), may hold values from -6 to 6
- output_cot: bfloat16 [128, 256, 768], P(('dp', 'mp')), may hold values from -6 to 6
- hidden_act: bfloat16 [128, 3072, 256], P('dp', 'mp'), may hold values from 0 to 2
- hidden_cot: bfloat16 [128, 3072, 256], P('dp', 'mp'), may hold values from -6 to 6
- lengths: int32 [128], P('dp'), may hold values from 32 to 256
- weights: float32 [768, 6144], P('dp', 'mp'), may hold values from -0.21875 to 0.21875
- moment_one: float32 [768, 6144], P('dp', 'mp'), may hold values from -3 to 3
- moment_two: float32 [768, 6144], P('dp', 'mp'), may hold values from 0.0005 to 0.02
Outputs:
- new_weights: float32 [768, 6144], P('dp', 'mp')
- new_moment_one: float32 [768, 6144], P('dp', 'mp')
- new_moment_two: float32 [768, 6144], P('dp', 'mp')
- clip_scale: float32 [128], P('dp')
Inputs may be any that keep to these rules, and one draw needn't show every extreme that they name: `lengths`: slots from an example's length on are padding.
All inputs are finite; a program needn't handle non-finite values.
Results may differ from a plain program's by a relative error of at most 0.0024.
Values may be sent and summed in bfloat16 or wider, within the bound.
A program may use at most 128 MiB of HBM per device.

v0:
```python
import math

import jax
import jax.numpy as jnp
from jax import lax
from jax.sharding import PartitionSpec as P

D = 768
FF = 3072
SLOT = 256
STEP = 10


beta_one = 0.9
beta_two = 0.999
adam_eps = 1e-08
learn_rate = 0.001
weight_decay = 0.01


def squared_norms(input_rows, outcot_rows, cot_rows, hid_rows):
    input_gram = jnp.einsum(
        "esd,etd->est", input_rows, input_rows, preferred_element_type=jnp.float32
    )
    cot_gram = jnp.einsum("efs,eft->est", cot_rows, cot_rows, preferred_element_type=jnp.float32)
    outcot_gram = jnp.einsum(
        "esd,etd->est", outcot_rows, outcot_rows, preferred_element_type=jnp.float32
    )
    hid_gram = jnp.einsum("efs,eft->est", hid_rows, hid_rows, preferred_element_type=jnp.float32)
    return jnp.sum(input_gram * cot_gram + outcot_gram * hid_gram, axis=(1, 2))


def clip_factor(squares):
    clip_limit = 0.5 * math.sqrt(2.0 * D * FF * SLOT)
    return clip_limit / jnp.maximum(jnp.sqrt(squares), clip_limit)


def masked_rows(own_lengths, hidden_cot, hidden_act):
    slot_index = lax.broadcasted_iota(jnp.int32, (own_lengths.shape[0], SLOT), 1)
    token_mask = (slot_index < own_lengths[:, None]).astype(jnp.float32)
    cot_masked = (hidden_cot.astype(jnp.float32) * token_mask[:, None, :]).astype(jnp.bfloat16)
    hid_masked = (hidden_act.astype(jnp.float32) * token_mask[:, None, :]).astype(jnp.bfloat16)
    return (token_mask, cot_masked, hid_masked)


def scaled_rows(clip_scale, token_mask, hidden_cot, hidden_act):
    factor = clip_scale[:, None] * token_mask
    scaled_cot = (hidden_cot.astype(jnp.float32) * factor[:, None, :]).astype(jnp.bfloat16)
    scaled_hid = (hidden_act.astype(jnp.float32) * factor[:, None, :]).astype(jnp.bfloat16)
    return (scaled_cot, scaled_hid)


def gradient_rows(input_rows, outcot_rows, cot_rows, hid_rows, row_count):
    contract = (((0, 1), (0, 2)), ((), ()))
    first_part = lax.dot_general(input_rows, cot_rows, contract, preferred_element_type=jnp.float32)
    second_part = lax.dot_general(
        outcot_rows, hid_rows, contract, preferred_element_type=jnp.float32
    )
    unit_count = cot_rows.shape[1]
    return jnp.stack([first_part, second_part], axis=2).reshape(row_count, 2 * unit_count)


def local(
    layer_input, output_cot, hidden_act, hidden_cot, lengths, weights, moment_one, moment_two
):
    local_examples = lengths.shape[0]
    input_full, outcot_full = (
        lax.all_gather(layer_input, "mp", axis=0, tiled=True),
        lax.all_gather(output_cot, "mp", axis=0, tiled=True),
    )
    token_mask, cot_masked, hid_masked = masked_rows(lengths, hidden_cot, hidden_act)
    partial_squares = squared_norms(input_full, outcot_full, cot_masked, hid_masked)
    squares = lax.psum(partial_squares, "mp")
    clip_scale = clip_factor(squares)
    scaled_cot, scaled_hid = scaled_rows(clip_scale, token_mask, hidden_cot, hidden_act)
    summed = lax.psum_scatter(
        gradient_rows(
            input_full,
            outcot_full,
            scaled_cot,
            scaled_hid,
            D // lax.axis_size("dp") * lax.axis_size("dp"),
        ).astype(jnp.bfloat16),
        "dp",
        scatter_dimension=0,
        tiled=True,
    ).astype(jnp.float32)
    gradient = summed / (local_examples * lax.axis_size("dp"))
    new_moment_one = beta_one * moment_one + (1.0 - beta_one) * gradient
    new_moment_two = beta_two * moment_two + (1.0 - beta_two) * gradient * gradient
    corr_one = 1.0 - beta_one**STEP
    corr_two = 1.0 - beta_two**STEP
    direction = new_moment_one / corr_one / (jnp.sqrt(new_moment_two / corr_two) + adam_eps)
    new_weights = weights - learn_rate * (direction + weight_decay * weights)
    return (new_weights, new_moment_one, new_moment_two, clip_scale)


def solution(mesh):
    return jax.shard_map(
        local,
        mesh=mesh,
        in_specs=(
            P(("dp", "mp"), None, None),
            P(("dp", "mp"), None, None),
            P("dp", "mp", None),
            P("dp", "mp", None),
            P("dp"),
            P("dp", "mp"),
            P("dp", "mp"),
            P("dp", "mp"),
        ),
        out_specs=(P("dp", "mp"), P("dp", "mp"), P("dp", "mp"), P("dp")),
        check_vma=False,
    )
```

profile of v0, /device:TPU:0, one launch (start us, length us, event | category | flops | bytes accessed | tf_op | source)
XLA Modules:
  0.0 470.0 jit_solution(956524610388416059)
XLA Ops:
  7.2 0.0 all-gather.5.cloned.1.call-start
  7.2 0.7 all-gather.5.cloned.1.call-update
  7.9 0.0 all-gather.3.cloned.1.call-start
  7.9 0.7 all-gather.3.cloned.1.call-update
  8.6 0.0 reduce-scatter.4.cloned.1.call-start
  8.7 0.7 fusion.40
  9.4 10.9 %fusion.6 = f32[32,256,256]{2,1,0:T(8,128)} fusion(bf16[32,384,256]{2,1,0:T(8,128)(2,1)} %param.10, f32[32,256]{1,0:T(8,128)S(1)} %fusion.40), kind=kOutput, calls=%fused_computation.10 | convolution fusion | flops 1620049920 | bytes 14712832 | tf_op jit(solution)/shard_map/efs,eft->est/dot_general | solution.py:29
  20.3 168.7 %all-gather.5.cloned.1.call-done = bf16[32,256,768]{2,1,0:T(8,128)(2,1)} async-done(((bf16[4,256,768]{2,1,0:T(8,128)(2,1)}), bf16[32,256,768]{2,1,0:T(8,128)(2,1)}) %all-gather.5.cloned.1.call-update) | async-done | bytes 12582928 | tf_op jit(solution)/shard_map/all_gather | solution.py:69
  189.0 16.7 %fusion.44 = f32[32,256,256]{2,1,0:T(8,128)} fusion(bf16[32,256,768]{2,1,0:T(8,128)(2,1)} %all-gather.5.cloned.1.call-done), kind=kOutput, calls=%fused_computation.36 | convolution fusion | flops 3221225472 | bytes 20971520 | tf_op jit(solution)/shard_map/esd,etd->est/dot_general | solution.py:26
  205.7 159.8 %all-gather.3.cloned.1.call-done = bf16[32,256,768]{2,1,0:T(8,128)(2,1)} async-done(((bf16[4,256,768]{2,1,0:T(8,128)(2,1)}), bf16[32,256,768]{2,1,0:T(8,128)(2,1)}) %all-gather.3.cloned.1.call-update) | async-done | bytes 12582928 | tf_op jit(solution)/shard_map/all_gather | solution.py:68
  365.5 16.5 %fusion.43 = f32[32,256,256]{2,1,0:T(8,128)} fusion(bf16[32,256,768]{2,1,0:T(8,128)(2,1)} %all-gather.3.cloned.1.call-done), kind=kOutput, calls=%fused_computation.35 | convolution fusion | flops 3221225472 | bytes 20971520 | tf_op jit(solution)/shard_map/esd,etd->est/dot_general | solution.py:22
  382.0 14.5 %add_reduce_fusion = f32[32]{0:T(128)S(1)} fusion(f32[32,256,256]{2,1,0:T(8,128)} %fusion.44, f32[32,256,256]{2,1,0:T(8,128)} %fusion.6, f32[32,256,256]{2,1,0:T(8,128)} %fusion.43, bf16[32,384,256]{2,1,0:T(8,128)(2,1)} %param.11, f32[32,256]{1,0:T(8,128)S(1)} %fusion.40), kind=kOutput, calls=%fused_computation.8 | convolution fusion | flops 1628438528 | bytes 31490176 | tf_op jit(solution)/shard_map/efs,eft->est/dot_general | solution.py:25
  396.5 18.7 %psum.7 = f32[32]{0:T(128)S(1)} all-reduce(f32[32]{0:T(128)S(1)} %add_reduce_fusion), channel_id=1, replica_groups=mesh['dp'=4,'mp'=8] {'mp'}, use_global_device_ids=true, to_apply=%region_1.0 | all-reduce | flops 32 | bytes 256 | tf_op jit(solution)/shard_map/psum | solution.py:73
  415.3 0.0 copy-start.3
  415.3 0.1 fusion.39
  415.3 11.0 %fusion.33 = bf16[768,384,1]{0,1,2:T(8,128)(2,1)S(1)} fusion(bf16[32,256,768]{2,1,0:T(8,128)(2,1)} %all-gather.5.cloned.1.call-done, bf16[32,384,256]{2,1,0:T(8,128)(2,1)} %param.10, f32[32,256]{1,0:T(8,128)S(1)} %fusion.39), kind=kOutput, calls=%fused_computation.22 | convolution fusion | flops 4841570304 | bytes 19496960 | tf_op jit(solution)/shard_map/dot_general | solution.py:56
  426.4 8.1 %fusion.30 = bf16[768,384,1]{0,1,2:T(8,128)(2,1)S(1)} fusion(bf16[32,256,768]{2,1,0:T(8,128)(2,1)} %all-gather.3.cloned.1.call-done, bf16[32,384,256]{2,1,0:T(8,128)(2,1)S(1)} %bitcast.30, f32[32,256]{1,0:T(8,128)S(1)} %fusion.39), kind=kOutput, calls=%fused_computation.21 | convolution fusion | flops 4841570304 | bytes 19496960 | tf_op jit(solution)/shard_map/dot_general | solution.py:55
  434.5 0.1 pad_maximum_fusion
  434.6 1.2 copy.36
  435.8 0.5 convert_element_type.41
  436.3 1.5 copy.40
  437.8 0.0 reduce-scatter.4.cloned.1.call-update
  437.8 23.0 %reduce-scatter.4.cloned.1.call-done = bf16[192,768]{1,0:T(8,128)(2,1)} async-done(((bf16[768,768]{1,0:T(8,128)(2,1)}), bf16[192,768]{1,0:T(8,128)(2,1)}) %reduce-scatter.4.cloned.1.call-update) | async-done | bytes 294928 | tf_op jit(solution)/shard_map/reduce_scatter | solution.py:76
  460.8 2.7 multiply_subtract_fusion
  (13 shorter events, 0.0 us)
Async XLA Ops:
  7.2 181.8 %all-gather.5.cloned.1.call-start = ((), (), s32[]{:S(2)}) async-start(), calls=%async_computation.2 | async-start | bytes 14155776 | tf_op jit(solution)/shard_map/all_gather | solution.py:69
  7.9 357.6 %all-gather.3.cloned.1.call-start = ((), (), s32[]{:S(2)}) async-start(), calls=%async_computation.1 | async-start | bytes 14155776 | tf_op jit(solution)/shard_map/all_gather | solution.py:68
  8.6 452.2 %reduce-scatter.4.cloned.1.call-start = ((), (), s32[]{:S(2)}) async-start(), calls=%async_computation.3 | async-start | bytes 1474560 | tf_op jit(solution)/shard_map/reduce_scatter | solution.py:76
  382.0 33.3 %copy-start.2 = (s32[32]{0:T(128)S(1)}, s32[32]{0:T(128)}, u32[]{:S(2)}) copy-start(s32[32]{0:T(128)} %param.12) | copy-start | bytes 388
  382.0 44.3 %slice-start = ((s8[6291456]{0:T(1024)(128)(4,1)}), s8[2097152]{0:T(1024)(128)(4,1)S(1)}, s32[]{:S(2)}) async-start(s8[6291456]{0:T(1024)(128)(4,1)} %bitcast.29), calls=%async_computation.4 | async-start | bytes 4194304
  415.3 11.1 %copy-start.3 = (f32[32]{0:T(128)}, f32[32]{0:T(128)S(1)}, u32[]{:S(2)}) copy-start(f32[32]{0:T(128)S(1)} %maximum_divide_fusion) | copy-start | bytes 388
  415.3 11.0 %slice-start.1 = ((s8[6291456]{0:T(1024)(128)(4,1)}), s8[4194304]{0:T(1024)(128)(4,1)S(1)}, s32[]{:S(2)}) async-start(s8[6291456]{0:T(1024)(128)(4,1)} %bitcast.29), calls=%async_computation.5 | async-start | bytes 8388608
  434.5 26.4 %copy-start = (f32[192,768]{1,0:T(8,128)S(1)}, f32[192,768]{1,0:T(8,128)}, u32[]{:S(2)}) copy-start(f32[192,768]{1,0:T(8,128)} %param.13) | copy-start | bytes 1769476
  434.5 26.4 %copy-start.1 = (f32[192,768]{1,0:T(8,128)S(1)}, f32[192,768]{1,0:T(8,128)}, u32[]{:S(2)}) copy-start(f32[192,768]{1,0:T(8,128)} %param.14) | copy-start | bytes 1769476
Sparse Core Ops, SparseCore 0:
  10.2 178.8 all-gather.4
  191.2 174.2 all-gather.2
  437.9 22.8 reduce-scatter.3
where the time goes:
time: 470 us
  waiting for transfers between devices  353 us (75%)
  matrix products  77.6 us (17%)
  blocking collectives  18.7 us (4%)
  between operations  13.8 us (3%)
    all_gather x1, waiting for transfers between devices, local(): lax.all_gather(output_cot, 'mp', axis=0, tiled=True)  169 us
    all_gather x1, waiting for transfers between devices, local(): lax.all_gather(layer_input, 'mp', axis=0, tiled=True)  160 us
    reduce_scatter x1, waiting for transfers between devices, local(): lax.psum_scatter(gradient_rows(input_full, outcot_full, scaled_cot, scale...  23 us
    psum x1, blocking collectives, local(): squares = lax.psum(partial_squares, 'mp')  18.7 us
    dot_general x1, matrix products, squared_norms(): jnp.einsum('esd,etd->est', outcot_rows, outcot_rows, preferred_element_ty...  16.7 us
    dot_general x1, matrix products, squared_norms(): jnp.einsum('esd,etd->est', input_rows, input_rows, preferred_element_type...  16.5 us
    dot_general x1, matrix products, squared_norms(): jnp.einsum('efs,eft->est', cot_rows, cot_rows, preferred_element_type=jnp...  14.5 us
    dot_general x1, matrix products, gradient_rows(): lax.dot_general(outcot_rows, hid_rows, contract, preferred_element_type=j...  11 us
  transfers between devices with their start and end apart: 3, of which 3 were waited for; matrix products, arithmetic and copies ran while one was open for 6% of the time, Pallas kernels for 0%

commit v1 on v0

v1 whole, which is shorter than its diff:
```python
import functools
import math

import jax
import jax.numpy as jnp
from jax import lax
from jax.experimental import pallas as pl
from jax.experimental.pallas import tpu as pltpu
from jax.sharding import PartitionSpec as P

STEP = 10

beta_one = 0.9
beta_two = 0.999
adam_eps = 1e-08
learn_rate = 0.001
weight_decay = 0.01

MESH = pl.DeviceIdType.MESH


def ring_order(count):
    fast = 1
    while fast * fast * 4 <= count and count % (fast * 2) == 0:
        fast *= 2
    slow = count // fast
    if fast == 1 or slow % 2:
        return list(range(count))
    walk = []
    for row in range(slow):
        columns = range(1, fast) if row % 2 == 0 else range(fast - 1, 0, -1)
        walk += [row * fast + column for column in columns]
    walk += [row * fast for row in range(slow - 1, -1, -1)]
    return walk


def pick(table, index):
    value = jnp.int32(table[0])
    for key in range(1, len(table)):
        value = jnp.where(index == key, jnp.int32(table[key]), value)
    return value


def kernel(
    dp,
    mp,
    clip_limit,
    input_ref,
    outcot_ref,
    cot_ref,
    hid_ref,
    mask_ref,
    grad_ref,
    clip_ref,
    input_all,
    outcot_all,
    products,
    x_buf,
    c_buf,
    sq_sum,
    sq_send,
    sq_all,
    total,
    arrived,
    ring_send,
    ring_recv,
    load_sem,
    sq_send_sem,
    sq_recv_sem,
    rs_send_sem,
    rs_recv_sem,
):
    own = input_ref.shape[0]
    examples, units = cot_ref.shape[0], cot_ref.shape[1]
    width = input_ref.shape[2]
    rows = grad_ref.shape[1]
    my_dp, my_mp = lax.axis_index("dp"), lax.axis_index("mp")
    order = ring_order(mp)
    place = [order.index(m) for m in range(mp)]
    pos = pick(place, my_mp)
    following = pick(order, lax.rem(pos + 1, mp))
    previous = pick(order, lax.rem(pos + mp - 1, mp))
    targets = (following, previous)
    own_refs = (input_ref, outcot_ref)
    all_refs = (input_all, outcot_all)
    hidden_refs = (cot_ref, hid_ref)

    barrier = pltpu.get_barrier_semaphore()
    for k in range(1, mp):
        peer = lax.rem(my_mp + k, mp)
        pl.semaphore_signal(barrier, inc=1, device_id=(my_dp, peer), device_id_type=MESH)
    for k in range(1, dp):
        peer = lax.rem(my_dp + k, dp)
        pl.semaphore_signal(barrier, inc=1, device_id=(peer, my_mp), device_id_type=MESH)
    pl.semaphore_wait(barrier, mp + dp - 2)

    def origins(step):
        return (
            pick(order, lax.rem(pos - step + mp, mp)),
            pick(order, lax.rem(pos + step, mp)),
        )

    def hop(k, source, example, step, chunk):
        return pltpu.make_async_remote_copy(
            src_ref=source,
            dst_ref=all_refs[k].at[example],
            send_sem=ring_send.at[k, step, chunk],
            recv_sem=ring_recv.at[k, step, chunk],
            device_id=(my_dp, targets[k]),
            device_id_type=MESH,
        )

    def load_hidden(k, example):
        return pltpu.make_async_copy(hidden_refs[k].at[example], c_buf.at[k], load_sem.at[k, 0])

    def load_rows(k, source):
        return pltpu.make_async_copy(source, x_buf.at[k], load_sem.at[k, 1])

    def product(k, example):
        mask = mask_ref[pl.ds(example, 1), :]
        masked = (c_buf[k].astype(jnp.float32) * mask).astype(jnp.bfloat16)
        piece = jnp.dot(masked, x_buf[k], preferred_element_type=jnp.float32)
        products[k, example] = piece.astype(jnp.bfloat16)
        sq_sum[pl.ds(example, 1), :] += jnp.sum(piece * piece, axis=0, keepdims=True)

    for chunk in range(own):
        for k in range(2):
            hop(k, own_refs[k].at[chunk], my_mp * own + chunk, 1, chunk).start()

    sq_sum[...] = jnp.zeros_like(sq_sum)

    def own_step(chunk, carry):
        example = my_mp * own + chunk
        for k in range(2):
            load_hidden(k, example).start()
            load_rows(k, own_refs[k].at[chunk]).start()
        for k in range(2):
            load_hidden(k, example).wait()
            load_rows(k, own_refs[k].at[chunk]).wait()
            product(k, example)
        return carry

    lax.fori_loop(0, own, own_step, 0)

    def ring_step(index, carry):
        step, chunk = lax.div(index, own), lax.rem(index, own)
        spots = [origin * own + chunk for origin in origins(step)]
        for k in range(2):
            load_hidden(k, spots[k]).start()
        for k in range(2):
            here = all_refs[k].at[spots[k]]
            hop(k, here, spots[k], step, chunk).wait_recv()

            @pl.when(step < mp - 1)
            def _():
                hop(k, here, spots[k], step + 1, chunk).start()

            load_rows(k, here).start()
        for k in range(2):
            load_hidden(k, spots[k]).wait()
            load_rows(k, all_refs[k].at[spots[k]]).wait()
            product(k, spots[k])
        return carry

    lax.fori_loop(own, mp * own, ring_step, 0)

    sums = jnp.broadcast_to(jnp.sum(sq_sum[...], axis=1, keepdims=True), sq_send.shape)
    sq_send[...] = sums
    sq_all[my_mp] = sums

    def share(k):
        return pltpu.make_async_remote_copy(
            src_ref=sq_send,
            dst_ref=sq_all.at[my_mp],
            send_sem=sq_send_sem.at[k],
            recv_sem=sq_recv_sem.at[k],
            device_id=(my_dp, lax.rem(my_mp + k, mp)),
            device_id_type=MESH,
        )

    for k in range(1, mp):
        share(k).start()

    def drain(index, carry):
        step, chunk = lax.div(index, own), lax.rem(index, own)
        for k in range(2):
            hop(k, own_refs[k].at[0], 0, step, chunk).wait_send()
        return carry

    lax.fori_loop(own, mp * own, drain, 0)
    for k in range(1, mp):
        share(k).wait()

    squares = sq_all[0]
    for source in range(1, mp):
        squares = squares + sq_all[source]
    clip_ref[...] = clip_limit / jnp.maximum(jnp.sqrt(squares), clip_limit)

    tile = 128
    unit_tile = tile if units % tile == 0 else units
    unit_tiles = units // unit_tile

    def scatter(k, ahead):
        peer = lax.rem(my_dp + ahead, dp)
        return pltpu.make_async_remote_copy(
            src_ref=total.at[k, pl.ds(pl.multiple_of(peer * rows, 16), rows), :],
            dst_ref=arrived.at[ahead, k],
            send_sem=rs_send_sem.at[k, ahead],
            recv_sem=rs_recv_sem.at[k, ahead],
            device_id=(peer, my_mp),
            device_id_type=MESH,
        )

    for k in range(2):

        def weigh(index, carry):
            column = pl.ds(pl.multiple_of(lax.div(index, unit_tiles) * tile, tile), tile)
            if unit_tiles == 1:
                unit = pl.ds(0, unit_tile)
            else:
                unit = pl.ds(pl.multiple_of(lax.rem(index, unit_tiles) * tile, tile), tile)
            value = jnp.zeros((unit_tile, tile), jnp.float32)
            for example in range(examples):
                value += clip_ref[example : example + 1, :] * products[
                    k, example, unit, column
                ].astype(jnp.float32)
            total[k, column, unit] = value.T.astype(jnp.bfloat16)
            return carry

        lax.fori_loop(0, width // tile * unit_tiles, weigh, 0)
        for ahead in range(1, dp):
            scatter(k, ahead).start()

    for k in range(2):
        grad = total[k, pl.ds(pl.multiple_of(my_dp * rows, 16), rows), :].astype(jnp.float32)
        for ahead in range(1, dp):
            scatter(k, ahead).wait()
            grad += arrived[ahead, k].astype(jnp.float32)
        grad_ref[k] = grad


def clipped_sum(dp, mp, layer_input, output_cot, hidden_cot, hidden_act, mask):
    own, slots, width = layer_input.shape
    examples, units, _ = hidden_cot.shape
    clip_limit = 0.5 * math.sqrt(2.0 * width * units * mp * slots)
    rows = width // dp
    anywhere = pl.BlockSpec(memory_space=pl.ANY)
    vmem = pl.BlockSpec(memory_space=pltpu.VMEM)
    dma = pltpu.SemaphoreType.DMA
    grad, clip, _, _ = pl.pallas_call(
        functools.partial(kernel, dp, mp, clip_limit),
        out_shape=(
            jax.ShapeDtypeStruct((2, rows, units), jnp.float32),
            jax.ShapeDtypeStruct((examples, 128), jnp.float32),
            jax.ShapeDtypeStruct((own * mp, slots, width), jnp.bfloat16),
            jax.ShapeDtypeStruct((own * mp, slots, width), jnp.bfloat16),
        ),
        in_specs=[anywhere] * 4 + [vmem],
        out_specs=(vmem, vmem, anywhere, anywhere),
        scratch_shapes=[
            pltpu.VMEM((2, examples, units, width), jnp.bfloat16),
            pltpu.VMEM((2, slots, width), jnp.bfloat16),
            pltpu.VMEM((2, units, slots), jnp.bfloat16),
            pltpu.VMEM((examples, width), jnp.float32),
            pltpu.VMEM((examples, 128), jnp.float32),
            pltpu.VMEM((mp, examples, 128), jnp.float32),
            pltpu.VMEM((2, width, units), jnp.bfloat16),
            pltpu.VMEM((dp, 2, rows, units), jnp.bfloat16),
            dma((2, mp, own)),
            dma((2, mp, own)),
            dma((2, 2)),
            dma((mp,)),
            dma((mp,)),
            dma((2, dp)),
            dma((2, dp)),
        ],
        compiler_params=pltpu.CompilerParams(
            collective_id=0, has_side_effects=True, vmem_limit_bytes=60 * 1024 * 1024
        ),
    )(layer_input, output_cot, hidden_cot, hidden_act, mask)
    return grad, clip


def local(
    dp, mp, layer_input, output_cot, hidden_act, hidden_cot, lengths, weights, moment_one, moment_two
):
    slots = layer_input.shape[1]
    slot_index = lax.broadcasted_iota(jnp.int32, (lengths.shape[0], slots), 1)
    mask = (slot_index < lengths[:, None]).astype(jnp.float32)
    summed, clip = clipped_sum(dp, mp, layer_input, output_cot, hidden_cot, hidden_act, mask)
    clip_scale = clip[:, 0]
    gradient = jnp.stack([summed[0], summed[1]], axis=2).reshape(weights.shape)
    gradient = gradient / (lengths.shape[0] * dp)
    new_moment_one = beta_one * moment_one + (1.0 - beta_one) * gradient
    new_moment_two = beta_two * moment_two + (1.0 - beta_two) * gradient * gradient
    corr_one = 1.0 - beta_one**STEP
    corr_two = 1.0 - beta_two**STEP
    direction = new_moment_one / corr_one / (jnp.sqrt(new_moment_two / corr_two) + adam_eps)
    new_weights = weights - learn_rate * (direction + weight_decay * weights)
    return (new_weights, new_moment_one, new_moment_two, clip_scale)


def solution(mesh):
    return jax.shard_map(
        functools.partial(local, mesh.shape["dp"], mesh.shape["mp"]),
        mesh=mesh,
        in_specs=(
            P(("dp", "mp"), None, None),
            P(("dp", "mp"), None, None),
            P("dp", "mp", None),
            P("dp", "mp", None),
            P("dp"),
            P("dp", "mp"),
            P("dp", "mp"),
            P("dp", "mp"),
        ),
        out_specs=(P("dp", "mp"), P("dp", "mp"), P("dp", "mp"), P("dp")),
        check_vma=False,
    )
```

time: 470 us -> 290 us (0.62)
  waiting for transfers between devices: 353 us -> 0 us
  Pallas kernels: 0 us -> 269 us
  matrix products: 77.6 us -> 0 us
  blocking collectives: 18.7 us -> 0 us
  between operations: 13.8 us -> 0.71 us
  local copies, waits for them, and re-layouts: 3.2 us -> 13.2 us
    all_gather x2 -> x0, waiting for transfers between devices: 329 us -> none  [the longest x1 169 us: local(): lax.all_gather(output_cot, 'mp', axis=0, tiled=True)]
    pallas_call x0 -> x1, Pallas kernels: none -> 269 us  [clipped_sum(): pl.pallas_call(functools.partial(kernel, dp, mp, clip_limit), out_shape=(...]
    dot_general x6 -> x0, matrix products: 77.6 us -> none  [the longest x1 16.7 us: squared_norms(): jnp.einsum('esd,etd->est', outcot_rows, outcot_rows, preferred_element_ty...]
    reduce_scatter x1 -> x0, waiting for transfers between devices: 23 us -> none  [local(): lax.psum_scatter(gradient_rows(input_full, outcot_full, scaled_cot, scale...]
    psum x1 -> x0, blocking collectives: 18.7 us -> none  [local(): squares = lax.psum(partial_squares, 'mp')]
    unnamed x13 -> x12, local copies, waits for them, and re-layouts: 1.49 us -> 8.91 us
  transfers between devices with their start and end apart: 3 -> 0, of which waited for: 3 -> 0; matrix products, arithmetic and copies ran while one was open for 6% -> 0% of each run, Pallas kernels for 0% -> 0%
where the time goes in v1:
time: 290 us; the launch traced here: 287 us
  Pallas kernels  269 us (93%)
  local copies, waits for them, and re-layouts  13.2 us (5%)
  other arithmetic  4.48 us (2%)
    pallas_call x1, Pallas kernels, clipped_sum(): pl.pallas_call(functools.partial(kernel, dp, mp, clip_limit), out_shape=(...  269 us
    unnamed x12, local copies, waits for them, and re-layouts  8.91 us

profile of v1, /device:TPU:0, one launch (start us, length us, event | category | flops | bytes accessed | tf_op | source)
XLA Modules:
  0.0 287.2 jit_solution(9561277263662880272)
XLA Ops:
  0.6 1.3 fusion.1.mask_ref
  2.0 268.8 %shard_map.111 = (f32[2,192,384]{2,1,0:T(8,128)}, f32[32,128]{1,0:T(8,128)}, bf16[32,256,768]{2,1,0:T(8,128)(2,1)}, bf16[32,256,768]{2,1,0:T(8,128)(2,1)}) custom-call(bf16[4,256,768]{2,1,0:T(8,128)(2,1)} %input_ref.1, bf16[4,256,768]{2,1,0:T(8,128)(2,1)} %outcot_ref.1, bf16[32,384,256]{2,1,0:T(8,128)(2,1)} %cot_ref.1, bf16[32,384,256]{2,1,0:T(8,128)(2,1)} %hid_ref.1, ...), custom_call_target="tpu_custom_call" | custom-call | tf_op jit(solution)/shard_map/pallas_call | solution.py:250
  270.8 0.0 copy-start
  270.8 0.0 copy-start.1
  270.8 1.2 slice_bitcast_fusion.1
  272.0 0.1 multiply_multiply_fusion
  272.1 0.7 copy.13
  272.8 0.5 mul.46
  273.4 0.7 copy.15
  274.1 0.5 mul.52
  274.6 0.0 copy-done
  274.6 1.2 copy.12
  275.8 0.0 copy-done.1
  275.8 0.0 copy-start.2
  275.8 1.2 copy.14
  277.0 2.2 copy.17
  279.2 3.0 %multiply_subtract_fusion = (f32[192,768]{0,1:T(8,128)}, f32[192,768]{0,1:T(8,128)S(1)}, f32[192,768]{0,1:T(8,128)S(1)}) fusion(f32[192,768]{0,1:T(8,128)} %copy.17, f32[192,768]{0,1:T(8,128)S(1)} %mul.46, f32[192,768]{0,1:T(8,128)} %copy.12, f32[192,768]{0,1:T(8,128)S(1)} %mul.52, f32[192,768]{0,1:T(8,128)} %copy.14), kind=kLoop, calls=%fused_computation | loop fusion | flops 1769472 | bytes 4718592 | tf_op jit(solution)/shard_map/sub | solution.py:299
  282.2 2.2 copy.18
  284.4 1.1 copy.19
  285.5 1.1 copy.20
  286.6 0.0 copy-done.2
  286.6 0.6 slice_reduce_fusion
Async XLA Ops:
  270.8 3.8 %copy-start = (f32[192,768]{1,0:T(8,128)S(1)}, f32[192,768]{1,0:T(8,128)}, u32[]{:S(2)}) copy-start(f32[192,768]{1,0:T(8,128)} %param.14) | copy-start | bytes 1769476
  270.8 5.0 %copy-start.1 = (f32[192,768]{1,0:T(8,128)S(1)}, f32[192,768]{1,0:T(8,128)}, u32[]{:S(2)}) copy-start(f32[192,768]{1,0:T(8,128)} %param.15) | copy-start | bytes 1769476
  275.8 10.8 %copy-start.2 = (f32[32,128]{1,0:T(8,128)S(1)}, f32[32,128]{1,0:T(8,128)}, u32[]{:S(2)}) copy-start(f32[32,128]{1,0:T(8,128)} %get-tuple-element.7) | copy-start | bytes 49156
